TPU v7x, 256 devices: a 4x2x16 block of a 4x16x16 slice. The times are simulated.
256 devices in a mesh: parts: 2 (over y), row: 16 (over z), chan: 4 (over x), sub: 2 (over core).
Axes of the slice: x: 4, y: 2, z: 16, core: 2. Of those that a mesh axis runs over, the one named last changes fastest.
The devices are a block of a 4x16x16 slice.
Arguments:
- pair: bfloat16 [896, 448, 128], P(('parts', 'row', 'sub'), 'chan'), parts along dimension 0, may hold values from -6 to 6
- pair_mask: int32 [896, 448], P(('parts', 'row', 'sub'), 'chan'), parts along dimension 0, may hold values 0 or 1
- out_in_gain: float32 [128], replicated, may hold values from 0.5 to 1.5
- out_proj: bfloat16 [128, 640], replicated, may hold values from -0.5 to 0.5
- out_mid_gain: float32 [128], replicated, may hold values from 0.5 to 1.5
- out_final: bfloat16 [128, 128], replicated, may hold values from -0.5 to 0.5
- in_in_gain: float32 [128], replicated, may hold values from 0.5 to 1.5
- in_proj: bfloat16 [128, 640], replicated, may hold values from -0.5 to 0.5
- in_mid_gain: float32 [128], replicated, may hold values from 0.5 to 1.5
- in_final: bfloat16 [128, 128], replicated, may hold values from -0.5 to 0.5
Outputs:
- updated: bfloat16 [896, 448, 128], P(('parts', 'row', 'sub'), 'chan'), parts along dimension 0
There are 2 independent parts, one for each index of `parts`. A program takes and returns all parts, laid end to end along the dimension named above; an argument that names none is the same for every part. Nothing has to cross between parts.
All inputs are finite; a program needn't handle non-finite values. No bound on the sum of `pair_mask` on one device may be relied on, other than what follows from the above.
Results may differ from a plain program's by a relative error of at most 0.014.
Values may be sent and summed in bfloat16 or wider, within the bound.
No kernel may reach another device: no remote copies, remote signals or barrier semaphores. Data moves between devices by JAX's collectives and lax.ppermute only.
A program may use at most 64 MiB of HBM per device.

v0:
```python
import jax
import jax.numpy as jnp
from jax import lax
from jax.sharding import PartitionSpec as P


def norm_last(values, gain):
    mean = jnp.mean(values, axis=-1, keepdims=True)
    var = jnp.mean((values - mean) ** 2, axis=-1, keepdims=True)
    return (values - mean) / jnp.sqrt(var + 1e-05) * gain


def norm_first(values, gain):
    mean = jnp.mean(values, axis=0, keepdims=True)
    var = jnp.mean((values - mean) ** 2, axis=0, keepdims=True)
    return (values - mean) / jnp.sqrt(var + 1e-05) * gain[:, None, None]


def project(pair, pair_mask, in_gain, proj, left_form, right_form, left_across):
    hidden = (proj.shape[1] - pair.shape[2]) // 4
    normed = norm_last(pair.astype(jnp.float32), in_gain).astype(jnp.bfloat16)
    keep = pair_mask.astype(jnp.float32)
    left_raw = jnp.einsum(
        left_form, normed, proj[:, : 2 * hidden], preferred_element_type=jnp.float32
    )
    right_raw = jnp.einsum(
        right_form, normed, proj[:, 2 * hidden : 4 * hidden], preferred_element_type=jnp.float32
    )
    left_keep = keep.T[None] if left_across else keep[None]
    left = (jax.nn.sigmoid(left_raw[:hidden]) * left_raw[hidden:] * left_keep).astype(jnp.bfloat16)
    right = (jax.nn.sigmoid(right_raw[:hidden]) * right_raw[hidden:] * keep[None]).astype(
        jnp.bfloat16
    )
    gate = jax.nn.sigmoid(
        jnp.dot(normed, proj[:, 4 * hidden :], preferred_element_type=jnp.float32)
    )
    return (left, right, gate)


def finish(pair, product, gate, mid_gain, final):
    whole = lax.all_to_all(
        product.astype(jnp.bfloat16), "chan", split_axis=2, concat_axis=0, tiled=True
    ).astype(product.dtype)
    normed = norm_first(whole, mid_gain).astype(jnp.bfloat16)
    update = jnp.einsum("crq,cd->rqd", normed, final, preferred_element_type=jnp.float32)
    return (pair.astype(jnp.float32) + gate * update).astype(jnp.bfloat16)


def shards(
    pair,
    pair_mask,
    out_in_gain,
    out_proj,
    out_mid_gain,
    out_final,
    in_in_gain,
    in_proj,
    in_mid_gain,
    in_final,
):
    left, right, gate = project(
        pair, pair_mask, out_in_gain, out_proj, "rqd,de->erq", "rqd,de->erq", False
    )
    left, right = (
        lax.all_to_all(left, "chan", split_axis=0, concat_axis=2, tiled=True),
        lax.all_to_all(right, "chan", split_axis=0, concat_axis=2, tiled=True),
    )
    product = jnp.einsum(
        "cik,cjk->cij",
        left,
        lax.all_gather(right, ("row", "sub"), axis=1, tiled=True),
        preferred_element_type=jnp.float32,
    )
    middle = finish(pair, product, gate, out_mid_gain, out_final)
    left_in, right_in, gate_in = project(
        middle, pair_mask, in_in_gain, in_proj, "rqd,de->eqr", "rqd,de->erq", True
    )
    columns = lax.all_to_all(
        lax.all_to_all(left_in, "chan", split_axis=0, concat_axis=1, tiled=True),
        ("row", "sub"),
        split_axis=1,
        concat_axis=2,
        tiled=True,
    )
    right_in = lax.all_to_all(right_in, "chan", split_axis=0, concat_axis=2, tiled=True)
    product_in = jnp.einsum(
        "cik,ckj->cij",
        columns,
        lax.all_gather(right_in, ("row", "sub"), axis=1, tiled=True),
        preferred_element_type=jnp.float32,
    )
    return finish(middle, product_in, gate_in, in_mid_gain, in_final)


def solution(mesh):
    placed = (
        P(("parts", "row", "sub"), "chan", None),
        P(("parts", "row", "sub"), "chan"),
        P(),
        P(),
        P(),
        P(),
        P(),
        P(),
        P(),
        P(),
    )
    return jax.shard_map(
        shards,
        mesh=mesh,
        in_specs=placed,
        out_specs=P(("parts", "row", "sub"), "chan", None),
        check_vma=False,
    )
```

profile of v0, /device:TPU:33, one launch (start us, length us, event | category | flops | bytes accessed | tf_op | source)
XLA Modules:
  0.0 357.3 jit_solution(9563343300795367324)
XLA Ops:
  9.4 1.7 convolution_bitcast_fusion.2
  13.5 11.9 %all_to_all.108 = bf16[128,14,112]{2,1,0:T(8,128)(2,1)S(1)} all-to-all(bf16[128,14,112]{2,1,0:T(8,128)(2,1)S(1)} %copy.93), channel_id=1, replica_groups=mesh['parts'=2,'row'=16,'chan'=4,'sub'=2] {'chan'}, dimensions={0} | all-to-all | bytes 802816 | tf_op jit(solution)/shard_map/all_to_all | solution.py:66
  27.3 9.4 %all_to_all.109 = bf16[128,14,112]{2,1,0:T(8,128)(2,1)S(1)} all-to-all(bf16[128,14,112]{2,1,0:T(8,128)(2,1)S(1)} %copy.90), channel_id=1, replica_groups=mesh['parts'=2,'row'=16,'chan'=4,'sub'=2] {'chan'}, dimensions={0} | all-to-all | bytes 802816 | tf_op jit(solution)/shard_map/all_to_all | solution.py:65
  37.5 98.7 %all-gather.3.cloned.1.call-done = bf16[32,448,448]{2,0,1:T(8,128)(2,1)} async-done(((bf16[32,14,448]{2,0,1:T(8,128)(2,1)}), bf16[32,448,448]{2,0,1:T(8,128)(2,1)}) %all-gather.3.cloned.1.call-update) | async-done | bytes 12845072 | tf_op jit(solution)/shard_map/all_gather | solution.py:71
  136.2 26.0 %fusion.12 = bf16[32,14,448]{2,1,0:T(8,128)(2,1)S(1)} fusion(bf16[32,14,448]{2,1,0:T(8,128)(2,1)S(1)} %reshape.80, bf16[32,448,448]{2,0,1:T(8,128)(2,1)} %all-gather.3.cloned.1.call-done), kind=kOutput, calls=%fused_computation.20 | convolution fusion | flops 180031488 | bytes 13647872 | tf_op jit(solution)/shard_map/cik,cjk->cij/dot_general | solution.py:68
  162.2 2.0 copy.98
  164.2 2.1 reshape.82
  166.4 4.0 %all-to-all-start.2 = ((bf16[4,2,25088]{2,1,0:T(2,128)(2,1)}), bf16[4,2,25088]{2,1,0:T(2,128)(2,1)S(1)}, u32[]{:S(2)}, u32[]{:S(2)}) async-start(bf16[4,2,25088]{2,1,0:T(2,128)(2,1)} %reshape.82), calls=%async_computation.2 | async-start | bytes 802816 | tf_op jit(solution)/shard_map/all_to_all | solution.py:41
  171.8 6.3 %all-to-all-done.2 = bf16[4,2,25088]{2,1,0:T(2,128)(2,1)S(1)} async-done(((bf16[4,2,25088]{2,1,0:T(2,128)(2,1)}), bf16[4,2,25088]{2,1,0:T(2,128)(2,1)S(1)}, u32[]{:S(2)}, u32[]{:S(2)}) %all-to-all-start.2) | async-done | bytes 401440 | tf_op jit(solution)/shard_map/all_to_all | solution.py:41
  179.5 1.6 copy.99
  185.4 10.3 %all_to_all.110 = bf16[128,14,112]{2,1,0:T(8,128)(2,1)S(1)} all-to-all(bf16[128,14,112]{2,1,0:T(8,128)(2,1)S(1)} %copy.108), channel_id=1, replica_groups=mesh['parts'=2,'row'=16,'chan'=4,'sub'=2] {'chan'}, dimensions={0} | all-to-all | bytes 802816 | tf_op jit(solution)/shard_map/all_to_all | solution.py:85
  198.3 9.4 %all_to_all.111 = bf16[128,112,14]{1,2,0:T(8,128)(2,1)S(1)} all-to-all(bf16[128,112,14]{1,2,0:T(8,128)(2,1)S(1)} %copy.102), channel_id=1, replica_groups=mesh['parts'=2,'row'=16,'chan'=4,'sub'=2] {'chan'}, dimensions={0} | all-to-all | bytes 802816 | tf_op jit(solution)/shard_map/all_to_all | solution.py:79
  207.6 1.6 copy.123
  210.7 45.8 %all_to_all.112 = bf16[32,2,3136]{2,1,0:T(2,128)(2,1)S(1)} all-to-all(bf16[32,2,3136]{2,1,0:T(2,128)(2,1)S(1)} %reshape.84), channel_id=1, replica_groups=mesh['parts'=2,'row'=16,'chan'=4,'sub'=2] {'row','sub'}, dimensions={0} | all-to-all | bytes 802816 | tf_op jit(solution)/shard_map/all_to_all | solution.py:78
  256.5 1.7 reshape.85
  258.2 4.7 %copy.126 = bf16[32,14,32,14]{3,2,1,0:T(8,128)(2,1)} copy(bf16[32,14,32,14]{0,3,1,2:T(8,128)(2,1)S(1)} %bitcast.105) | data formatting | bytes 802816 | tf_op jit(solution)/shard_map/all_to_all | solution.py:78
  262.9 7.3 %reshape.81 = bf16[32,14,448]{2,1,0:T(8,128)(2,1)S(1)} reshape(bf16[32,14,32,14]{3,2,1,0:T(8,128)(2,1)} %copy.126) | data formatting | bytes 802816 | tf_op jit(solution)/shard_map/all_to_all | solution.py:78
  270.2 37.5 %all-gather.5.cloned.1.call-done = bf16[32,448,448]{2,0,1:T(8,128)(2,1)} async-done(((bf16[32,14,448]{2,0,1:T(8,128)(2,1)}), bf16[32,448,448]{2,0,1:T(8,128)(2,1)}) %all-gather.5.cloned.1.call-update) | async-done | bytes 12845072 | tf_op jit(solution)/shard_map/all_gather | solution.py:89
  307.7 20.7 %fusion.15 = bf16[32,14,448]{2,1,0:T(8,128)(2,1)S(1)} fusion(bf16[32,14,448]{2,1,0:T(8,128)(2,1)S(1)} %reshape.81, bf16[32,448,448]{2,0,1:T(8,128)(2,1)} %all-gather.5.cloned.1.call-done), kind=kOutput, calls=%fused_computation.21 | convolution fusion | flops 180031488 | bytes 13647872 | tf_op jit(solution)/shard_map/cik,ckj->cij/dot_general | solution.py:86
  330.0 2.1 reshape.86
  332.1 4.0 %all-to-all-start.6 = ((bf16[4,2,25088]{2,1,0:T(2,128)(2,1)}), bf16[4,2,25088]{2,1,0:T(2,128)(2,1)S(1)}, u32[]{:S(2)}, u32[]{:S(2)}) async-start(bf16[4,2,25088]{2,1,0:T(2,128)(2,1)} %reshape.86), calls=%async_computation.6 | async-start | bytes 802816 | tf_op jit(solution)/shard_map/all_to_all | solution.py:41
  336.1 2.0 fusion.7
  338.1 5.7 %all-to-all-done.6 = bf16[4,2,25088]{2,1,0:T(2,128)(2,1)S(1)} async-done(((bf16[4,2,25088]{2,1,0:T(2,128)(2,1)}), bf16[4,2,25088]{2,1,0:T(2,128)(2,1)S(1)}, u32[]{:S(2)}, u32[]{:S(2)}) %all-to-all-start.6) | async-done | bytes 401440 | tf_op jit(solution)/shard_map/all_to_all | solution.py:41
  345.2 1.6 copy.114
  (82 shorter events, 25.0 us)
Async XLA Ops:
  6.5 176.1 %copy-start = (bf16[128,128]{1,0:T(8,128)(2,1)S(1)}, bf16[128,128]{1,0:T(8,128)(2,1)}, u32[]{:S(2)}) copy-start(bf16[128,128]{1,0:T(8,128)(2,1)} %param.15) | copy-start | bytes 98308
  6.6 129.7 %all-gather.3.cloned.1.call-start = ((), (), s32[]{:S(2)}) async-start(), calls=%async_computation.7 | async-start | bytes 15138816 | tf_op jit(solution)/shard_map/all_gather | solution.py:71
  9.3 1.7 copy-start.2
  9.3 1.7 copy-start.14
  9.4 3.2 copy-start.9
  11.1 1.5 copy-start.8
  164.2 6.2 %copy-start.10 = (f32[14,112]{1,0:T(8,128)S(1)}, f32[14,112]{1,0:T(8,128)}, u32[]{:S(2)}) copy-start(f32[14,112]{1,0:T(8,128)} %copy-done.9) | copy-start | bytes 18820
  164.2 6.1 %copy-start.15 = (f32[128]{0:T(128)S(1)}, f32[128]{0:T(128)}, u32[]{:S(2)}) copy-start(f32[128]{0:T(128)} %param.12) | copy-start | bytes 1540
  166.4 11.7 %all-to-all-start.2 = ((bf16[4,2,25088]{2,1,0:T(2,128)(2,1)}), bf16[4,2,25088]{2,1,0:T(2,128)(2,1)S(1)}, u32[]{:S(2)}, u32[]{:S(2)}) async-start(bf16[4,2,25088]{2,1,0:T(2,128)(2,1)} %reshape.82), calls=%async_computation.2 | async-start | bytes 802816 | tf_op jit(solution)/shard_map/all_to_all | solution.py:41
  170.4 137.3 %all-gather.5.cloned.1.call-start = ((), (), s32[]{:S(2)}) async-start(), calls=%async_computation.8 | async-start | bytes 15138816 | tf_op jit(solution)/shard_map/all_gather | solution.py:89
  181.8 0.7 copy-start.11
  182.6 1.1 copy-start.13
  182.6 1.6 copy-start.6
  184.3 12.9 %copy-start.3 = (bf16[14,112,128]{2,1,0:T(8,128)(2,1)}, bf16[14,112,128]{2,1,0:T(8,128)(2,1)S(1)}, u32[]{:S(2)}) copy-start(bf16[14,112,128]{2,1,0:T(8,128)(2,1)S(1)} %multiply_convert_fusion) | copy-start | bytes 1204228
  329.9 6.1 %copy-start.4 = (bf16[14,112,128]{2,1,0:T(8,128)(2,1)S(1)}, bf16[14,112,128]{2,1,0:T(8,128)(2,1)}, u32[]{:S(2)}) copy-start(bf16[14,112,128]{2,1,0:T(8,128)(2,1)} %copy-done.3) | copy-start | bytes 1204228
  332.1 11.7 %all-to-all-start.6 = ((bf16[4,2,25088]{2,1,0:T(2,128)(2,1)}), bf16[4,2,25088]{2,1,0:T(2,128)(2,1)S(1)}, u32[]{:S(2)}, u32[]{:S(2)}) async-start(bf16[4,2,25088]{2,1,0:T(2,128)(2,1)} %reshape.86), calls=%async_computation.6 | async-start | bytes 802816 | tf_op jit(solution)/shard_map/all_to_all | solution.py:41
  347.5 0.7 copy-start.12
  348.0 1.1 copy-start.5
  348.0 1.1 copy-start.7
  348.0 2.2 copy-start.1
Sparse Core Ops, SparseCore 0:
  27.0 109.2 all-gather.2
  197.3 110.3 all-gather.4
where the time goes:
time: 362 us; the launch traced here: 357 us
  waiting for transfers between devices  148 us (41%)
  blocking collectives  86.7 us (24%)
  matrix products  55.5 us (15%)
  local copies, waits for them, and re-layouts  38.5 us (11%)
  between operations  14.2 us (4%)
  starting transfers between devices  7.98 us (2%)
  other arithmetic  6.1 us (2%)
    all_gather x1, waiting for transfers between devices, shards(): lax.all_gather(right, ('row', 'sub'), axis=1, tiled=True)  98.7 us
    all_to_all x1, blocking collectives, shards(): lax.all_to_all(lax.all_to_all(left_in, 'chan', split_axis=0, concat_axis=...  45.8 us
    all_gather x1, waiting for transfers between devices, shards(): lax.all_gather(right_in, ('row', 'sub'), axis=1, tiled=True)  37.5 us
    dot_general x1, matrix products, shards(): jnp.einsum('cik,cjk->cij', left, lax.all_gather(right, ('row', 'sub'), ax...  26 us
    dot_general x1, matrix products, shards(): jnp.einsum('cik,ckj->cij', columns, lax.all_gather(right_in, ('row', 'sub...  20.7 us
    all_to_all x2, local copies, waits for them, and re-layouts, shards(): lax.all_to_all(lax.all_to_all(left_in, 'chan', split_axis=0, concat_axis=...  12 us
    all_to_all x2, waiting for transfers between devices, finish(): lax.all_to_all(product.astype(jnp.bfloat16), 'chan', split_axis=2, concat...  12 us
    all_to_all x1, blocking collectives, shards(): lax.all_to_all(right, 'chan', split_axis=0, concat_axis=2, tiled=True)  11.9 us
  transfers between devices with their start and end apart: 4, of which 4 were waited for; matrix products, arithmetic and copies ran while one was open for 6% of the time, Pallas kernels for 0%

commit v1 on v0

--- a/solution.py
+++ b/solution.py
@@ -2,6 +2,14 @@
 import jax.numpy as jnp
 from jax import lax
 from jax.sharding import PartitionSpec as P
+
+
+def gather_by_exchange(value, axis, dim):
+    peers = lax.axis_size(axis)
+    repeats = [peers if d == dim else 1 for d in range(value.ndim)]
+    return lax.all_to_all(
+        jnp.tile(value, repeats), axis, split_axis=dim, concat_axis=dim, tiled=True
+    )
 
 
 def norm_last(values, gain):
@@ -86,7 +94,7 @@
     product_in = jnp.einsum(
         "cik,ckj->cij",
         columns,
-        lax.all_gather(right_in, ("row", "sub"), axis=1, tiled=True),
+        gather_by_exchange(right_in, ("row", "sub"), 1),
         preferred_element_type=jnp.float32,
     )
     return finish(middle, product_in, gate_in, in_mid_gain, in_final)

time: 362 us -> 953 us (2.63); the launches traced: 357 us -> 936 us
  waiting for transfers between devices: 148 us -> 755 us
  blocking collectives: 86.7 us -> 21.2 us
  starting transfers between devices: 7.98 us -> 33.4 us
  local copies, waits for them, and re-layouts: 38.5 us -> 50.1 us
    all_to_all x0 -> x4, waiting for transfers between devices: none -> 645 us  [the longest x1 609 us: gather_by_exchange(): lax.all_to_all(jnp.tile(value, repeats), axis, split_axis=dim, concat_axi...]
    all_to_all x3 -> x0, blocking collectives: 65.5 us -> none  [the longest x1 45.8 us: shards(): lax.all_to_all(lax.all_to_all(left_in, 'chan', split_axis=0, concat_axis=...]
    all_gather x1 -> x0, waiting for transfers between devices: 37.5 us -> none  [shards(): lax.all_gather(right_in, ('row', 'sub'), axis=1, tiled=True)]
    all_to_all x0 -> x4, starting transfers between devices: none -> 25.8 us  [the longest x1 12.9 us: shards(): lax.all_to_all(lax.all_to_all(left_in, 'chan', split_axis=0, concat_axis=...]
  transfers between devices with their start and end apart: 4 -> 7, of which waited for: 4 -> 7; matrix products, arithmetic and copies ran while one was open for 6% -> 3% of each run, Pallas kernels for 0% -> 0%
where the time goes in v1:
time: 953 us; the launch traced here: 936 us
  waiting for transfers between devices  755 us (79%)
  matrix products  55.6 us (6%)
  local copies, waits for them, and re-layouts  50.1 us (5%)
  starting transfers between devices  33.4 us (4%)
  blocking collectives  21.2 us (2%)
  between operations  14.2 us (1%)
    all_to_all x1, waiting for transfers between devices, gather_by_exchange(): lax.all_to_all(jnp.tile(value, repeats), axis, split_axis=dim, concat_axi...  609 us
    all_gather x1, waiting for transfers between devices, shards(): lax.all_gather(right, ('row', 'sub'), axis=1, tiled=True)  98.7 us
    all_to_all x1, waiting for transfers between devices, shards(): lax.all_to_all(lax.all_to_all(left_in, 'chan', split_axis=0, concat_axis=...  27.5 us
    dot_general x1, matrix products, shards(): jnp.einsum('cik,cjk->cij', left, lax.all_gather(right, ('row', 'sub'), ax...  26.8 us
    dot_general x1, matrix products, shards(): jnp.einsum('cik,ckj->cij', columns, gather_by_exchange(right_in, ('row',...  20.7 us
  transfers between devices with their start and end apart: 7, of which 7 were waited for; matrix products, arithmetic and copies ran while one was open for 3% of the time, Pallas kernels for 0%

profile of v1, /device:TPU:33, one launch (start us, length us, event | category | flops | bytes accessed | tf_op | source)
XLA Modules:
  0.0 935.8 jit_solution(14139698481598518937)
XLA Ops:
  12.7 11.9 %all_to_all.110 = bf16[128,14,112]{2,1,0:T(8,128)(2,1)S(1)} all-to-all(bf16[128,14,112]{2,1,0:T(8,128)(2,1)S(1)} %copy.92), channel_id=1, replica_groups=mesh['parts'=2,'row'=16,'chan'=4,'sub'=2] {'chan'}, dimensions={0} | all-to-all | bytes 802816 | tf_op jit(solution)/shard_map/all_to_all | solution.py:74
  26.5 9.4 %all_to_all.111 = bf16[128,14,112]{2,1,0:T(8,128)(2,1)S(1)} all-to-all(bf16[128,14,112]{2,1,0:T(8,128)(2,1)S(1)} %copy.89), channel_id=1, replica_groups=mesh['parts'=2,'row'=16,'chan'=4,'sub'=2] {'chan'}, dimensions={0} | all-to-all | bytes 802816 | tf_op jit(solution)/shard_map/all_to_all | solution.py:73
  36.7 98.7 %all-gather.2.cloned.1.call-done = bf16[32,448,448]{2,0,1:T(8,128)(2,1)} async-done(((bf16[32,14,448]{2,0,1:T(8,128)(2,1)}), bf16[32,448,448]{2,0,1:T(8,128)(2,1)}) %all-gather.2.cloned.1.call-update) | async-done | bytes 12845072 | tf_op jit(solution)/shard_map/all_gather | solution.py:79
  135.4 26.8 %fusion.12 = bf16[32,14,448]{2,1,0:T(8,128)(2,1)} fusion(bf16[32,14,448]{2,1,0:T(8,128)(2,1)S(1)} %reshape.85, bf16[32,448,448]{2,0,1:T(8,128)(2,1)} %all-gather.2.cloned.1.call-done), kind=kOutput, calls=%fused_computation.20 | convolution fusion | flops 180031488 | bytes 13647872 | tf_op jit(solution)/shard_map/cik,cjk->cij/dot_general | solution.py:76
  162.2 3.1 copy.97
  165.3 2.1 reshape.87
  167.5 4.0 all-to-all-start.2
  173.0 6.2 all-to-all-done.2
  187.9 3.6 all-to-all-start.3
  193.4 5.9 all-to-all-done.3
  199.3 3.6 all-to-all-start.5
  202.9 2.7 copy.122
  205.6 2.1 reshape.89
  209.7 12.9 %all-to-all-start.4 = ((bf16[32,2,3136]{2,1,0:T(2,128)(2,1)}), bf16[32,2,3136]{2,1,0:T(2,128)(2,1)S(1)}, u32[]{:S(2)}, u32[]{:S(2)}) async-start(bf16[32,2,3136]{2,1,0:T(2,128)(2,1)} %reshape.89), calls=%async_computation.4 | async-start | bytes 819200 | tf_op jit(solution)/shard_map/all_to_all | solution.py:86
  223.3 27.5 %all-to-all-done.4 = bf16[32,2,3136]{2,1,0:T(2,128)(2,1)S(1)} async-done(((bf16[32,2,3136]{2,1,0:T(2,128)(2,1)}), bf16[32,2,3136]{2,1,0:T(2,128)(2,1)S(1)}, u32[]{:S(2)}, u32[]{:S(2)}) %all-to-all-start.4) | async-done | bytes 401440 | tf_op jit(solution)/shard_map/all_to_all | solution.py:86
  250.8 7.0 tile.12
  257.8 5.8 all-to-all-start.6
  265.3 4.7 copy.125
  270.1 7.3 reshape.86
  277.4 609.3 %all-to-all-done.6 = bf16[32,448,448]{2,0,1:T(8,128)(2,1)} async-done(((bf16[32,448,448]{2,0,1:T(8,128)(2,1)}), bf16[32,448,448]{2,0,1:T(8,128)(2,1)}, u32[]{:S(2)}, u32[]{:S(2)}) %all-to-all-start.6) | async-done | bytes 12845088 | tf_op jit(solution)/shard_map/all_to_all | solution.py:10
  886.7 20.7 %fusion.15 = bf16[32,14,448]{2,1,0:T(8,128)(2,1)S(1)} fusion(bf16[32,14,448]{2,1,0:T(8,128)(2,1)S(1)} %reshape.86, bf16[32,448,448]{2,0,1:T(8,128)(2,1)} %all-to-all-done.6), kind=kOutput, calls=%fused_computation.21 | convolution fusion | flops 180031488 | bytes 13647872 | tf_op jit(solution)/shard_map/cik,ckj->cij/dot_general | solution.py:94
  908.9 2.1 reshape.91
  911.1 3.6 all-to-all-start.7
  916.7 5.6 all-to-all-done.7
  (89 shorter events, 35.0 us)
Async XLA Ops:
  6.5 177.1 %copy-start = (bf16[128,128]{1,0:T(8,128)(2,1)S(1)}, bf16[128,128]{1,0:T(8,128)(2,1)}, u32[]{:S(2)}) copy-start(bf16[128,128]{1,0:T(8,128)(2,1)} %param.15) | copy-start | bytes 98308
  6.6 128.9 %all-gather.2.cloned.1.call-start = ((), (), s32[]{:S(2)}) async-start(), calls=%async_computation.8 | async-start | bytes 15138816 | tf_op jit(solution)/shard_map/all_gather | solution.py:79
  9.3 1.7 copy-start.2
  9.3 1.7 copy-start.16
  9.4 1.7 copy-start.17
  11.1 0.7 copy-start.12
  167.5 11.7 %all-to-all-start.2 = ((bf16[4,2,25088]{2,1,0:T(2,128)(2,1)}), bf16[4,2,25088]{2,1,0:T(2,128)(2,1)S(1)}, u32[]{:S(2)}, u32[]{:S(2)}) async-start(bf16[4,2,25088]{2,1,0:T(2,128)(2,1)} %reshape.87), calls=%async_computation.2 | async-start | bytes 802816 | tf_op jit(solution)/shard_map/all_to_all | solution.py:49
  182.8 0.7 copy-start.13
  183.3 1.1 copy-start.8
  184.5 1.1 copy-start.15
  184.5 1.6 copy-start.10
  186.1 5.4 copy-start.3
  187.9 11.3 %all-to-all-start.3 = ((bf16[128,112,14]{1,2,0:T(8,128)(2,1)}), bf16[128,112,14]{1,2,0:T(8,128)(2,1)S(1)}, u32[]{:S(2)}, u32[]{:S(2)}) async-start(bf16[128,112,14]{1,2,0:T(8,128)(2,1)} %copy.101), calls=%async_computation.3 | async-start | bytes 1048576 | tf_op jit(solution)/shard_map/all_to_all | solution.py:87
  199.3 3.6 copy-start.5
  199.3 10.4 %all-to-all-start.5 = ((bf16[128,14,112]{2,1,0:T(8,128)(2,1)}), bf16[128,14,112]{2,1,0:T(8,128)(2,1)S(1)}, u32[]{:S(2)}, u32[]{:S(2)}) async-start(bf16[128,14,112]{2,1,0:T(8,128)(2,1)} %copy.107), calls=%async_computation.5 | async-start | bytes 1048576 | tf_op jit(solution)/shard_map/all_to_all | solution.py:93
  209.7 41.1 %all-to-all-start.4 = ((bf16[32,2,3136]{2,1,0:T(2,128)(2,1)}), bf16[32,2,3136]{2,1,0:T(2,128)(2,1)S(1)}, u32[]{:S(2)}, u32[]{:S(2)}) async-start(bf16[32,2,3136]{2,1,0:T(2,128)(2,1)} %reshape.89), calls=%async_computation.4 | async-start | bytes 819200 | tf_op jit(solution)/shard_map/all_to_all | solution.py:86
  250.8 7.0 copy-start.6
  257.8 5.8 copy-start.7
  257.8 628.8 %all-to-all-start.6 = ((bf16[32,448,448]{2,0,1:T(8,128)(2,1)}), bf16[32,448,448]{2,0,1:T(8,128)(2,1)}, u32[]{:S(2)}, u32[]{:S(2)}) async-start(bf16[32,448,448]{2,0,1:T(8,128)(2,1)} %bitcast.99), calls=%async_computation.6 | async-start | bytes 29360128 | tf_op jit(solution)/shard_map/all_to_all | solution.py:10
  908.9 5.7 copy-start.4
  911.1 11.2 %all-to-all-start.7 = ((bf16[4,2,25088]{2,1,0:T(2,128)(2,1)}), bf16[4,2,25088]{2,1,0:T(2,128)(2,1)S(1)}, u32[]{:S(2)}, u32[]{:S(2)}) async-start(bf16[4,2,25088]{2,1,0:T(2,128)(2,1)} %reshape.91), calls=%async_computation.7 | async-start | bytes 802816 | tf_op jit(solution)/shard_map/all_to_all | solution.py:49
  926.5 1.1 copy-start.9
  926.5 1.1 copy-start.11
  926.5 2.2 copy-start.1
  (1 other events, 0.7 us)
Sparse Core Ops, SparseCore 0:
  26.2 109.2 all-gather.1
